TPU v7x, 256 devices: a whole 4x4x8 slice. The times are simulated.
256 devices in a mesh: row: 32 (over y, x, core), col: 8 (over z).
Axes of the slice: x: 4, y: 4, z: 8, core: 2. Of those that a mesh axis runs over, the one named last changes fastest.
Arguments:
- integrals: bfloat16 [1280, 32, 8192], P('row', None, 'col'), may hold values from -6 to 6
- coeffs: bfloat16 [40960, 4096], P('row', 'col'), may hold values from -0.0546875 to 0.0546875
- mask: int32 [1280, 8], replicated, may hold values from 0 to 1, as said below
- offsets: int32 [1281], replicated, may hold values from 0 to 30720, as said below
- atom_of_slot: int32 [1280], replicated, may hold values from 0 to 1279, as said below
Outputs:
- half_transformed: bfloat16 [4096, 8192], P('row', 'col')
Inputs may be any that keep to these rules, and one draw needn't show every extreme that they name: `mask`: 1 marks a significant pair of an atom and a block of 64 window functions. offsets[0] = 0 and offsets[a + 1] - offsets[a] is atom a's number of basis functions, 16 to 32; atoms 2k and 2k + 1 together have 3 * 16; rows of an atom's padded block past its number are padding. `atom_of_slot`: a permutation of the atoms; slot k is held by atom owner k // 40 along row, and atom a's AO-row owner is a // 40; one atom owner holds at least one and at most 2 atoms of any one AO-row owner, and exactly 2 for some pairs.
All inputs are finite; a program needn't handle non-finite values.
Results may differ from a plain program's by a relative error of at most 0.015.
Values may be sent and summed in bfloat16 or wider, within the bound.
A program may use at most 256 MiB of HBM per device.

v0:
```python
import jax
import jax.numpy as jnp
from jax import lax
from jax.sharding import PartitionSpec as P


def body(integrals, coeffs, mask, offsets, atom_of_slot):
    n_row = lax.axis_size("row")
    own_row = lax.axis_index("row")
    own_col = lax.axis_index("col")
    per_dev, atom_w, row_width = integrals.shape
    slots_cap = max(2, -(-per_dev // n_row))
    counter = jnp.arange(per_dev, dtype=jnp.int32)
    slot_count = n_row * slots_cap
    mine_slots = lax.dynamic_slice_in_dim(atom_of_slot, own_row * per_dev, per_dev)
    target = mine_slots // per_dev
    before = (target[None, :] == target[:, None]) & (counter[None, :] < counter[:, None])
    arrival_rank = jnp.sum(before.astype(jnp.int32), axis=1)
    position = target * slots_cap + arrival_rank
    placing = (jnp.arange(slot_count, dtype=jnp.int32)[:, None] == position[None, :]).astype(
        jnp.bfloat16
    )
    outgoing = jnp.dot(
        placing, integrals.reshape(per_dev, atom_w * row_width), preferred_element_type=jnp.bfloat16
    )
    outgoing = outgoing.reshape(n_row, slots_cap, atom_w * row_width)
    incoming = lax.all_to_all(outgoing, "row", split_axis=0, concat_axis=0, tiled=True)
    holders = atom_of_slot.reshape(n_row, per_dev)
    is_mine = holders // per_dev == own_row
    arrival = jnp.cumsum(is_mine.astype(jnp.int32), axis=1) - 1
    slot_of = jnp.arange(n_row, dtype=jnp.int32)[:, None] * slots_cap + arrival
    local_atom = holders - own_row * per_dev
    pick_atom = (
        (local_atom.reshape(-1)[:, None] == counter[None, :]) & is_mine.reshape(-1)[:, None]
    ).astype(jnp.float32)
    pick_slot = (
        slot_of.reshape(-1)[:, None] == jnp.arange(slot_count, dtype=jnp.int32)[None, :]
    ).astype(jnp.float32)
    gather_matrix = jnp.dot(pick_atom.T, pick_slot).astype(jnp.bfloat16)
    ordered = jnp.dot(
        gather_matrix,
        incoming.reshape(slot_count, atom_w * row_width),
        preferred_element_type=jnp.bfloat16,
    )
    ordered = ordered.reshape(per_dev, atom_w, row_width)
    bounds = lax.dynamic_slice_in_dim(offsets, own_row * per_dev, per_dev + 1)
    lengths = bounds[1:] - bounds[:-1]
    significant = lax.dynamic_slice(mask, (own_row * per_dev, own_col), (per_dev, 1))[:, 0] > 0
    keep_rows = (jnp.arange(atom_w, dtype=jnp.int32)[None, :] < lengths[:, None]) & significant[
        :, None
    ]
    blocks = ordered * keep_rows[:, :, None].astype(jnp.bfloat16)
    bucket_edges = [0, per_dev]
    kept_rows = blocks.reshape(per_dev * atom_w, row_width)
    coeff_piece = lax.all_gather(coeffs, "col", axis=1, tiled=True)
    low_row = bucket_edges[0] * atom_w
    high_row = bucket_edges[1] * atom_w

    def product(low_row=low_row, high_row=high_row):
        return lax.dot_general(
            coeff_piece, kept_rows, (((0,), (0,)), ((), ())), preferred_element_type=jnp.float32
        )

    bucket_term = product()
    partial_sums = bucket_term.astype(jnp.bfloat16)
    result = lax.psum_scatter(partial_sums, "row", scatter_dimension=0, tiled=True).astype(
        jnp.float32
    )
    return result.astype(jnp.bfloat16)


def solution(mesh):
    in_specs = (P("row", None, "col"), P("row", "col"), P(), P(), P())
    out_specs = P("row", "col")
    return jax.shard_map(body, mesh=mesh, in_specs=in_specs, out_specs=out_specs, check_vma=False)
```

profile of v0, /device:TPU:2, one launch (start us, length us, event | category | flops | bytes accessed | tf_op | source)
XLA Modules:
  0.0 260.2 jit_solution(1185108357489608472)
XLA Ops:
  6.5 0.7 all-gather.2.cloned.1.call-update
  7.3 5.3 %reshape.121 = bf16[40,32768,1]{1,0,2:T(8,128)(2,1)} reshape(bf16[40,32,1024]{2,1,0:T(8,128)(2,1)} %param.5) | data formatting | bytes 5242880 | tf_op jit(solution)/shard_map/reshape | solution.py:24
  12.6 0.1 and_select_fusion
  12.6 0.2 convert_reduce_fusion
  12.8 0.1 multiply_add_fusion.1
  12.9 3.0 %fusion.17 = bf16[32,2,32768]{2,0,1:T(8,128)(2,1)S(1)} fusion(bf16[40,32768,1]{1,0,2:T(8,128)(2,1)} %reshape.121, s32[40]{0:T(128)S(1)} %multiply_add_fusion.1, s32[32,2]{0,1:T(2,128)S(1)} %multiply_add_fusion), kind=kOutput, calls=%fused_computation.13 | convolution fusion | flops 167774720 | bytes 6816160 | tf_op jit(solution)/shard_map/dot_general | solution.py:23
  16.0 6.3 %copy.15 = bf16[32,2,32768]{2,1,0:T(2,128)(2,1)} copy(bf16[32,2,32768]{2,0,1:T(8,128)(2,1)S(1)} %fusion.17) | data formatting | bytes 8388608 | tf_op jit(solution)/shard_map/dot_general | solution.py:23
  22.2 7.7 %all-to-all-start = ((bf16[32,2,32768]{2,1,0:T(2,128)(2,1)}), bf16[32,2,32768]{2,1,0:T(2,128)(2,1)}, u32[]{:S(2)}, u32[]{:S(2)}) async-start(bf16[32,2,32768]{2,1,0:T(2,128)(2,1)} %copy.15), calls=%async_computation | async-start | bytes 8388608 | tf_op jit(solution)/shard_map/all_to_all | solution.py:27
  29.9 0.2 reduce-scatter.4.cloned.1.call-start
  30.2 0.1 and.41
  30.3 0.1 div.18
  30.4 0.2 reduce_window_sum.11
  30.6 0.1 add_add_fusion
  30.7 0.1 add.46
  30.7 0.8 dynamic_slice.10
  31.5 0.8 compare_bitcast_fusion
  32.4 49.0 %all-to-all-done = bf16[32,2,32768]{2,1,0:T(2,128)(2,1)} async-done(((bf16[32,2,32768]{2,1,0:T(2,128)(2,1)}), bf16[32,2,32768]{2,1,0:T(2,128)(2,1)}, u32[]{:S(2)}, u32[]{:S(2)}) %all-to-all-start) | async-done | bytes 4194336 | tf_op jit(solution)/shard_map/all_to_all | solution.py:27
  81.3 7.2 %reshape.119 = bf16[64,32768]{1,0:T(8,128)(2,1)} reshape(bf16[32,2,32768]{2,1,0:T(2,128)(2,1)} %all-to-all-done) | data formatting | bytes 8388608 | tf_op jit(solution)/shard_map/reshape | solution.py:42
  88.6 3.9 %fusion.3 = bf16[40,32,1024]{2,0,1:T(8,128)(2,1)S(1)} fusion(bf16[8,32,8,1024]{3,2,1,0:T(8,128)(2,1)} %bitcast.20, bf16[40,32]{0,1:T(8,128)(2,1)S(1)} %fusion.24, s32[1280]{0:T(1024)S(1)} %add.46, s32[1280]{0:T(1024)S(1)} %get-tuple-element.7, pred[1280]{0:T(1024)(128)(4,1)S(1)} %get-tuple-element.5), kind=kOutput, calls=%fused_computation.4 | convolution fusion | flops 179755520 | bytes 6829824 | tf_op jit(solution)/shard_map/dot_general | solution.py:40
  92.5 2.9 %copy.17 = bf16[40,32,1024]{2,1,0:T(8,128)(2,1)} copy(bf16[40,32,1024]{2,0,1:T(8,128)(2,1)S(1)} %fusion.3) | data formatting | bytes 5242880 | tf_op jit(solution)/shard_map/mul | solution.py:52
  95.4 30.4 %all-gather.2.cloned.1.call-done = bf16[1280,4096]{1,0:T(8,128)(2,1)} async-done(((bf16[1280,512]{1,0:T(8,128)(2,1)}), bf16[1280,4096]{1,0:T(8,128)(2,1)}) %all-gather.2.cloned.1.call-update) | async-done | bytes 10485776 | tf_op jit(solution)/shard_map/all_gather | solution.py:55
  125.8 16.8 %convert_bitcast_fusion = bf16[4096,1024]{0,1:T(8,128)(2,1)} fusion(bf16[1280,1024]{1,0:T(8,128)(2,1)} %bitcast.21, bf16[1280,4096]{1,0:T(8,128)(2,1)} %all-gather.2.cloned.1.call-done), kind=kOutput, calls=%fused_computation | convolution fusion | flops 10741612544 | bytes 21495808 | tf_op jit(solution)/shard_map/dot_general | solution.py:60
  142.6 12.0 %copy.19 = bf16[4096,1024]{1,0:T(8,128)(2,1)} copy(bf16[4096,1024]{0,1:T(8,128)(2,1)} %convert_bitcast_fusion) | data formatting | bytes 16777216
  154.6 98.8 %reduce-scatter.4.cloned.1.call-done = bf16[128,1024]{1,0:T(8,128)(2,1)} async-done(((bf16[4096,1024]{1,0:T(8,128)(2,1)}), bf16[128,1024]{1,0:T(8,128)(2,1)}) %reduce-scatter.4.cloned.1.call-update) | async-done | bytes 262160 | tf_op jit(solution)/shard_map/reduce_scatter | solution.py:66
  (11 shorter events, 0.1 us)
Async XLA Ops:
  6.5 6.0 %copy-start = (s32[1280]{0:T(1024)S(1)}, s32[1280]{0:T(1024)}, u32[]{:S(2)}) copy-start(s32[1280]{0:T(1024)} %param.9) | copy-start | bytes 15364
  6.5 119.3 %all-gather.2.cloned.1.call-start = ((), (), s32[]{:S(2)}) async-start(), calls=%async_computation.2 | async-start | bytes 11796480 | tf_op jit(solution)/shard_map/all_gather | solution.py:55
  22.2 59.1 %all-to-all-start = ((bf16[32,2,32768]{2,1,0:T(2,128)(2,1)}), bf16[32,2,32768]{2,1,0:T(2,128)(2,1)}, u32[]{:S(2)}, u32[]{:S(2)}) async-start(bf16[32,2,32768]{2,1,0:T(2,128)(2,1)} %copy.15), calls=%async_computation | async-start | bytes 8388608 | tf_op jit(solution)/shard_map/all_to_all | solution.py:27
  29.9 223.5 %reduce-scatter.4.cloned.1.call-start = ((), (), s32[]{:S(2)}) async-start(), calls=%async_computation.3 | async-start | bytes 8650752 | tf_op jit(solution)/shard_map/reduce_scatter | solution.py:66
Sparse Core Ops, SparseCore 0:
  9.1 116.6 all-gather.1
  154.7 98.6 reduce-scatter.3
where the time goes:
time: 261 us; the launch traced here: 260 us
  waiting for transfers between devices  179 us (69%)
  local copies, waits for them, and re-layouts  34.7 us (13%)
  matrix products  23.7 us (9%)
  between operations  13.5 us (5%)
  starting transfers between devices  7.9 us (3%)
    reduce_scatter x1, waiting for transfers between devices, body(): lax.psum_scatter(partial_sums, 'row', scatter_dimension=0, tiled=True)  98.8 us
    all_to_all x1, waiting for transfers between devices, body(): lax.all_to_all(outgoing, 'row', split_axis=0, concat_axis=0, tiled=True)  49 us
    all_gather x1, waiting for transfers between devices, body(): coeff_piece = lax.all_gather(coeffs, 'col', axis=1, tiled=True)  30.4 us
    dot_general x1, matrix products, product(): lax.dot_general(coeff_piece, kept_rows, (((0,), (0,)), ((), ())), preferr...  16.8 us
    unnamed x3, local copies, waits for them, and re-layouts  12 us
    all_to_all x1, starting transfers between devices, body(): lax.all_to_all(outgoing, 'row', split_axis=0, concat_axis=0, tiled=True)  7.68 us
    reshape x1, local copies, waits for them, and re-layouts, body(): incoming.reshape(slot_count, atom_w * row_width)  7.23 us
    dot_general x1, local copies, waits for them, and re-layouts, body(): jnp.dot(placing, integrals.reshape(per_dev, atom_w * row_width), preferre...  6.28 us
  transfers between devices with their start and end apart: 3, of which 3 were waited for; matrix products, arithmetic and copies ran while one was open for 12% of the time, Pallas kernels for 0%

commit v1 on v0

--- a/solution.py
+++ b/solution.py
@@ -52,7 +52,16 @@
     blocks = ordered * keep_rows[:, :, None].astype(jnp.bfloat16)
     bucket_edges = [0, per_dev]
     kept_rows = blocks.reshape(per_dev * atom_w, row_width)
-    coeff_piece = lax.all_gather(coeffs, "col", axis=1, tiled=True)
+    name_views = lambda local_array: jnp.concatenate(
+        lax.all_to_all(
+            jnp.stack([local_array for _ in range(lax.axis_size("col"))]),
+            axis_name="col",
+            split_axis=0,
+            concat_axis=0,
+        ),
+        axis=1,
+    )
+    coeff_piece = name_views(coeffs)
     low_row = bucket_edges[0] * atom_w
     high_row = bucket_edges[1] * atom_w
 

time: 261 us -> 458 us (1.75)
  waiting for transfers between devices: 179 us -> 361 us
  starting transfers between devices: 7.9 us -> 16.6 us
  local copies, waits for them, and re-layouts: 34.7 us -> 39.8 us
    all_to_all x0 -> x1, waiting for transfers between devices: none -> 215 us  [body(): lax.all_to_all(jnp.stack([local_array for _ in range(lax.axis_size('col')...]
    all_gather x1 -> x0, waiting for transfers between devices: 30.4 us -> none  [body(): coeff_piece = lax.all_gather(coeffs, 'col', axis=1, tiled=True)]
    all_to_all x0 -> x1, starting transfers between devices: none -> 8.6 us  [body(): lax.all_to_all(jnp.stack([local_array for _ in range(lax.axis_size('col')...]
    unnamed x3 -> x6, local copies, waits for them, and re-layouts: 12 us -> 12.6 us
  transfers between devices with their start and end apart: 3 -> 3, of which waited for: 3 -> 3; matrix products, arithmetic and copies ran while one was open for 12% -> 4% of each run, Pallas kernels for 0% -> 0%
where the time goes in v1:
time: 458 us; the launch traced here: 457 us
  waiting for transfers between devices  361 us (79%)
  local copies, waits for them, and re-layouts  39.8 us (9%)
  matrix products  23.6 us (5%)
  starting transfers between devices  16.6 us (4%)
  between operations  13.5 us (3%)
    all_to_all x1, waiting for transfers between devices, body(): lax.all_to_all(jnp.stack([local_array for _ in range(lax.axis_size('col')...  215 us
    reduce_scatter x1, waiting for transfers between devices, body(): lax.psum_scatter(partial_sums, 'row', scatter_dimension=0, tiled=True)  95.1 us
    all_to_all x1, waiting for transfers between devices, body(): lax.all_to_all(outgoing, 'row', split_axis=0, concat_axis=0, tiled=True)  50.8 us
    dot_general x1, matrix products, product(): lax.dot_general(coeff_piece, kept_rows, (((0,), (0,)), ((), ())), preferr...  16.7 us
    unnamed x6, local copies, waits for them, and re-layouts  12.6 us
  transfers between devices with their start and end apart: 3, of which 3 were waited for; matrix products, arithmetic and copies ran while one was open for 4% of the time, Pallas kernels for 0%

profile of v1, /device:TPU:2, one launch (start us, length us, event | category | flops | bytes accessed | tf_op | source)
XLA Modules:
  0.0 457.3 jit_solution(12801380798418694993)
XLA Ops:
  6.5 0.8 and_select_fusion
  7.3 0.2 convert_reduce_fusion
  7.5 0.8 multiply_add_fusion.1
  8.3 5.3 %reshape.131 = bf16[40,32768,1]{1,0,2:T(8,128)(2,1)} reshape(bf16[40,32,1024]{2,1,0:T(8,128)(2,1)} %param.5) | data formatting | bytes 5242880 | tf_op jit(solution)/shard_map/reshape | solution.py:24
  13.5 3.0 fusion.17
  16.6 6.2 %copy.17 = bf16[32,2,32768]{2,1,0:T(2,128)(2,1)} copy(bf16[32,2,32768]{2,0,1:T(8,128)(2,1)S(1)} %fusion.17) | data formatting | bytes 8388608 | tf_op jit(solution)/shard_map/dot_general | solution.py:23
  22.8 7.8 %all-to-all-start = ((bf16[32,2,32768]{2,1,0:T(2,128)(2,1)}), bf16[32,2,32768]{2,1,0:T(2,128)(2,1)}, u32[]{:S(2)}, u32[]{:S(2)}) async-start(bf16[32,2,32768]{2,1,0:T(2,128)(2,1)} %copy.17), calls=%async_computation | async-start | bytes 8388608 | tf_op jit(solution)/shard_map/all_to_all | solution.py:27
  30.7 0.6 copy.20
  31.3 50.8 %all-to-all-done = bf16[32,2,32768]{2,1,0:T(2,128)(2,1)} async-done(((bf16[32,2,32768]{2,1,0:T(2,128)(2,1)}), bf16[32,2,32768]{2,1,0:T(2,128)(2,1)}, u32[]{:S(2)}, u32[]{:S(2)}) %all-to-all-start) | async-done | bytes 4194336 | tf_op jit(solution)/shard_map/all_to_all | solution.py:27
  82.1 4.5 stack.2
  86.6 8.6 %all-to-all-start.1 = ((bf16[8,1280,512]{1,2,0:T(8,128)(2,1)}), bf16[8,1280,512]{1,2,0:T(8,128)(2,1)}, u32[]{:S(2)}, u32[]{:S(2)}) async-start(bf16[8,1280,512]{1,2,0:T(8,128)(2,1)} %stack.2), calls=%async_computation.1 | async-start | bytes 20971520 | tf_op jit(solution)/shard_map/all_to_all | solution.py:56
  95.2 0.2 reduce-scatter.4.cloned.1.call-start
  95.4 0.1 and.41
  95.6 0.2 reduce_window_sum.11
  95.9 0.1 add.46
  96.0 0.8 dynamic_slice.10
  96.8 0.8 compare_bitcast_fusion
  97.6 7.2 %reshape.127 = bf16[64,32768]{1,0:T(8,128)(2,1)} reshape(bf16[32,2,32768]{2,1,0:T(2,128)(2,1)} %all-to-all-done) | data formatting | bytes 8388608 | tf_op jit(solution)/shard_map/reshape | solution.py:42
  104.9 3.9 fusion.3
  108.8 3.0 copy.19
  111.7 215.0 %all-to-all-done.1 = bf16[8,1280,512]{1,2,0:T(8,128)(2,1)} async-done(((bf16[8,1280,512]{1,2,0:T(8,128)(2,1)}), bf16[8,1280,512]{1,2,0:T(8,128)(2,1)}, u32[]{:S(2)}, u32[]{:S(2)}) %all-to-all-start.1) | async-done | bytes 10485792 | tf_op jit(solution)/shard_map/all_to_all | solution.py:56
  326.8 16.7 %convert_bitcast_fusion = bf16[4096,1024]{0,1:T(8,128)(2,1)} fusion(bf16[1280,1024]{1,0:T(8,128)(2,1)} %bitcast.24, bf16[1280,4096]{0,1:T(8,128)(2,1)} %bitcast.5), kind=kOutput, calls=%fused_computation | convolution fusion | flops 10741612544 | bytes 21495808 | tf_op jit(solution)/shard_map/dot_general | solution.py:69
  343.4 12.0 %copy.22 = bf16[4096,1024]{1,0:T(8,128)(2,1)} copy(bf16[4096,1024]{0,1:T(8,128)(2,1)} %convert_bitcast_fusion) | data formatting | bytes 16777216
  355.4 95.1 %reduce-scatter.4.cloned.1.call-done = bf16[128,1024]{1,0:T(8,128)(2,1)} async-done(((bf16[4096,1024]{1,0:T(8,128)(2,1)}), bf16[128,1024]{1,0:T(8,128)(2,1)}) %reduce-scatter.4.cloned.1.call-update) | async-done | bytes 262160 | tf_op jit(solution)/shard_map/reduce_scatter | solution.py:75
  (14 shorter events, 0.3 us)
Async XLA Ops:
  22.8 7.8 %copy-start = (bf16[1280,512]{1,0:T(8,128)(2,1)S(1)}, bf16[1280,512]{1,0:T(8,128)(2,1)}, u32[]{:S(2)}) copy-start(bf16[1280,512]{1,0:T(8,128)(2,1)} %param.6) | copy-start | bytes 3932164
  22.8 59.2 %all-to-all-start = ((bf16[32,2,32768]{2,1,0:T(2,128)(2,1)}), bf16[32,2,32768]{2,1,0:T(2,128)(2,1)}, u32[]{:S(2)}, u32[]{:S(2)}) async-start(bf16[32,2,32768]{2,1,0:T(2,128)(2,1)} %copy.17), calls=%async_computation | async-start | bytes 8388608 | tf_op jit(solution)/shard_map/all_to_all | solution.py:27
  86.6 8.8 %copy-start.1 = (s32[1280]{0:T(1024)S(1)}, s32[1280]{0:T(1024)}, u32[]{:S(2)}) copy-start(s32[1280]{0:T(1024)} %param.9) | copy-start | bytes 15364
  86.6 240.2 %all-to-all-start.1 = ((bf16[8,1280,512]{1,2,0:T(8,128)(2,1)}), bf16[8,1280,512]{1,2,0:T(8,128)(2,1)}, u32[]{:S(2)}, u32[]{:S(2)}) async-start(bf16[8,1280,512]{1,2,0:T(8,128)(2,1)} %stack.2), calls=%async_computation.1 | async-start | bytes 20971520 | tf_op jit(solution)/shard_map/all_to_all | solution.py:56
  95.2 355.3 %reduce-scatter.4.cloned.1.call-start = ((), (), s32[]{:S(2)}) async-start(), calls=%async_computation.3 | async-start | bytes 8650752 | tf_op jit(solution)/shard_map/reduce_scatter | solution.py:75
Sparse Core Ops, SparseCore 0:
  355.6 94.8 reduce-scatter.3
